TPU v7x, 32 devices: a whole 2x2x4 slice. The times are simulated.
32 devices in a mesh: grp: 4 (over z), dev: 8 (over y, x, core).
Axes of the slice: x: 2, y: 2, z: 4, core: 2. Of those that a mesh axis runs over, the one named last changes fastest.
Arguments:
- atm_state: float32 [4, 8, 128, 1024], P('grp', 'dev'), may hold values from -6 to 6
- atm_nbrs: int32 [4, 8, 4, 1024], P('grp', 'dev'), may hold values from 0 to 1279
- atm_send: int32 [4, 8, 256], P('grp', 'dev'), may hold values from 0 to 1023
- atm_mix: float32 [4, 8, 1024], P('grp', 'dev'), may hold values from 0.2 to 0.6
- flux_weight: float32 [24, 128], replicated, may hold values from -0.5 to 0.5
- margin_counts: int32 [4, 8, 1024], P('grp', 'dev'), may hold values from 1 to 4, 1536 in all within a row
- margin_weight: float32 [4, 8, 1536], P('grp', 'dev'), may hold values from 0.05 to 1
- block_owner: int32 [4, 8, 12, 1], P('grp', 'dev'), may hold values from 0 to 1, as said below
- recv_cols: int32 [4, 8, 2, 12, 128], P('grp', 'dev'), may hold values from 0 to 2047
- ocn_state: float32 [4, 8, 80, 2048], P('grp', 'dev'), may hold values from -6 to 6
- ocn_nbrs: int32 [4, 8, 6, 2048], P('grp', 'dev'), may hold values from 0 to 2303
- ocn_send: int32 [4, 8, 256], P('grp', 'dev'), may hold values from 0 to 2047
- ocn_mix: float32 [4, 8, 2048], P('grp', 'dev'), may hold values from 0.1 to 0.4
- force_weight: float32 [80, 24], replicated, may hold values from -1.25 to 1.25
- ret_weight: float32 [12, 80], replicated, may hold values from -0.625 to 0.625
Outputs:
- atm_next: float32 [4, 8, 128, 1024], P('grp', 'dev')
- ocn_next: float32 [4, 8, 80, 2048], P('grp', 'dev')
- atm_remapped: float32 [4, 8, 12, 1024], P('grp', 'dev')
Inputs may be any that keep to these rules, and one draw needn't show every extreme that they name: `margin_counts`: the 1024 counts of one partition sum to 1536, and one of them equals 4. `block_owner`: no partition sends more than 12 of its 12 blocks to one ocean group, and every partition sends exactly 12 blocks to one of them.
All inputs are finite; a program needn't handle non-finite values.
Results may differ from a plain program's by a relative error of at most 0.0029.
Values may be sent and summed in bfloat16 or wider, within the bound.
A program may use at most 64 MiB of HBM per device.

v0:
```python
import functools

import jax
import jax.numpy as jnp
from jax import lax
from jax.experimental import pallas as pl
from jax.experimental.pallas import tpu as pltpu
from jax.sharding import PartitionSpec as P

EXACT = lax.Precision.HIGHEST
BF = jnp.bfloat16
F32 = jnp.float32
I32 = jnp.int32
NT = (((1,), (1,)), ((), ()))
TN = (((0,), (0,)), ((), ()))


def mm(a, b):
    return jnp.dot(a, b, preferred_element_type=F32)


def two_parts(x):
    rest = x - x.astype(BF).astype(F32)
    return jnp.concatenate([x, rest], axis=0).astype(BF)


def joined(x):
    half = x.shape[0] // 2
    return x[:half] + x[half:]


def low_hot(low, t):
    place = lax.broadcasted_iota(I32, low.shape, 0).astype(F32).astype(BF)
    return jnp.where(low - jnp.asarray(16.0 * t, BF) == place, jnp.asarray(1, BF), jnp.asarray(0, BF))


def as_rows(idx, rows):
    return jnp.broadcast_to(idx.astype(F32), (rows, idx.shape[1])).astype(BF)


def hot_rows(high, h, rows):
    return jnp.where(jnp.broadcast_to(high, (rows, high.shape[1])) == h, 1.0, 0.0).astype(BF)


def one_hot(idx, rows, base):
    width = idx.shape[1]
    place = lax.broadcasted_iota(I32, (rows, width), 0) + base
    return jnp.where(place == idx, 1.0, 0.0).astype(BF)


def counts_matrix(out_ref, high_ref, idx_rows, base, at):
    width = idx_rows[0].shape[1]
    highs = out_ref.shape[0] // base
    bits = base.bit_length() - 1
    low = [as_rows(i & (base - 1), 16) for i in idx_rows]
    for k, i in enumerate(idx_rows):
        for h in range(highs):
            high_ref[k * highs + h, :, :width] = hot_rows(i >> bits, h, 16)
    for t in range(base // 16):
        parts = [low_hot(i, t) for i in low]
        for h in range(highs):
            total = parts[0] * high_ref[h, :, :width]
            for k in range(1, len(parts)):
                total = total + parts[k] * high_ref[k * highs + h, :, :width]
            out_ref[pl.ds(h * base + t * 16, 16), at] = total


def base_of(length):
    return 256 if length % 256 == 0 else 128


def row_columns(counts, rows):
    lines = counts.shape[0]
    wide = jnp.concatenate([counts.astype(F32), jnp.zeros((-lines % 16, 128), F32)], axis=0).astype(BF)
    lines = wide.shape[0]
    i = lax.broadcasted_iota(I32, (128, 128), 0)
    j = lax.broadcasted_iota(I32, (128, 128), 1)
    within = mm(wide, jnp.where(i <= j, 1.0, 0.0).astype(BF))
    i = lax.broadcasted_iota(I32, (lines, lines), 0)
    j = lax.broadcasted_iota(I32, (lines, lines), 1)
    ones = jnp.ones((128, 128), BF)
    before = mm(mm(jnp.where(j < i, 1.0, 0.0).astype(BF), wide).astype(BF), ones)
    upto = mm(mm(jnp.where(j <= i, 1.0, 0.0).astype(BF), wide).astype(BF), ones)
    offsets = within + before
    high = jnp.floor(offsets * (1.0 / 256.0)) * 256.0
    halves = jnp.concatenate([high, offsets - high], axis=0).astype(BF)
    tiles = rows // 128
    at = lax.broadcasted_iota(I32, (lines, rows), 1).astype(F32)
    ends = jnp.concatenate([upto] * tiles, axis=1)
    starts = jnp.concatenate([before] * tiles, axis=1)
    passed = jnp.where(ends <= at, 1.0, 0.0)
    line = jnp.where(starts <= at, 1.0, 0.0) - passed
    line = jnp.concatenate([line, line], axis=0).astype(BF)
    ends_in = lax.dot_general(halves, line, TN, preferred_element_type=F32)
    at = lax.broadcasted_iota(I32, (128, rows), 1).astype(F32)
    inner = jnp.sum(jnp.where(ends_in <= at, 1.0, 0.0), axis=0, keepdims=True)
    return 128.0 * jnp.sum(passed, axis=0, keepdims=True) + inner


def kernel(
    sizes,
    air_hbm, anbr_hbm, asend_hbm, amix_hbm, fw_hbm, counts_hbm, mw_hbm, owner_hbm,
    recv_hbm, sea_hbm, onbr_hbm, osend_hbm, omix_hbm, force_hbm, retw_hbm,
    air_out, sea_out, back_out,
    anbr, asend, amix, fw, counts, mw, owner, recv, onbr, osend, omix, force, retw_in,
    pack, halo, apool, gpool, opool, amat, omat0, omat1, member, lowmat, lowrow, spread, high, high1,
    codes_out, codes_in, up_out, up_in, down_out, down_in, retw, slab, ret_bf, wide_force,
    load, halo_send, halo_recv, code_send, code_recv, up_send, relay_send, up_recv, down_send, down_recv,
):
    groups, devs, air_groups = sizes
    sea_groups = groups - air_groups
    g, d = lax.axis_index("grp"), lax.axis_index("dev")
    lower, upper = lax.rem(d + devs - 1, devs), lax.rem(d + 1, devs)
    is_air = g < air_groups
    mine = jnp.where(is_air, g, g - air_groups)
    half = halo.shape[2]
    capacity, block = recv.shape[2], recv.shape[4]
    span = capacity * block
    levels_a, columns = air_out.shape[2:]
    levels_o, cells = sea_out.shape[2:]
    fields = fw.shape[0]
    ret_fields = retw_in.shape[0]
    ret_pad = retw.shape[0]
    blocks = owner.shape[3]
    row_count = mw.shape[2]
    pairs = blocks // 2
    same = capacity == blocks
    base = lowmat.shape[0]
    bits = base.bit_length() - 1
    highs = cells // base
    field_pad = spread.shape[0] // highs
    width = high.shape[2]

    barrier = pltpu.get_barrier_semaphore()
    pl.semaphore_signal(barrier, inc=1, device_id={"dev": lower})
    pl.semaphore_signal(barrier, inc=1, device_id={"dev": upper})

    loads = [
        pltpu.make_async_copy(a, b, load.at[i])
        for i, (a, b) in enumerate((
            (air_hbm, air_out), (anbr_hbm, anbr), (asend_hbm, asend), (amix_hbm, amix), (fw_hbm, fw),
            (counts_hbm, counts), (mw_hbm, mw), (owner_hbm, owner), (recv_hbm, recv), (sea_hbm, sea_out),
            (onbr_hbm, onbr), (osend_hbm, osend), (omix_hbm, omix), (force_hbm, force), (retw_hbm, retw_in),
        ))
    ]
    (l_air, l_anbr, l_asend, l_amix, l_fw, l_counts, l_mw, l_owner,
     l_recv, l_sea, l_onbr, l_osend, l_omix, l_force, l_retw) = loads

    def halos(levels):
        return [
            pltpu.make_async_remote_copy(
                src_ref=pack.at[1 - side, :levels], dst_ref=halo.at[side, :levels],
                send_sem=halo_send.at[side], recv_sem=halo_recv.at[side],
                device_id={"dev": upper if side == 0 else lower})
            for side in range(2)
        ]

    def code_copy(s, o):
        return pltpu.make_async_remote_copy(
            src_ref=codes_out, dst_ref=codes_in.at[s], send_sem=code_send.at[o],
            recv_sem=code_recv.at[s], device_id={"grp": air_groups + o})

    def up_copy(s, p):
        return pltpu.make_async_remote_copy(
            src_ref=up_out.at[p], dst_ref=up_in.at[s, p], send_sem=up_send.at[p],
            recv_sem=up_recv.at[s, p], device_id={"grp": air_groups})

    def relay_copy(s, p):
        return pltpu.make_async_remote_copy(
            src_ref=up_in.at[s, p], dst_ref=up_in.at[s, p], send_sem=relay_send.at[s, p],
            recv_sem=up_recv.at[s, p], device_id={"grp": g + 1})

    def down_copy(s, o):
        return pltpu.make_async_remote_copy(
            src_ref=down_out.at[s], dst_ref=down_in.at[o], send_sem=down_send.at[s],
            recv_sem=down_recv.at[o], device_id={"grp": s})

    def packed(state_ref, send_ref, pool):
        levels, length = state_ref.shape[2:]
        top = state_ref[0, 0].astype(BF)
        pool[:, :length] = top
        chosen = mm(top, one_hot(send_ref[0], length, 0)).astype(BF)
        pack[0, :levels, :] = chosen[:, :half]
        pack[1, :levels, :] = chosen[:, half:]

    def take_halo(copies, pool, levels, length):
        for c in copies:
            c.wait()
        for side in range(2):
            at = slice(length + side * half, length + (side + 1) * half)
            pool[:, at] = halo[side, :levels, :]

    @pl.when(is_air)
    def _():
        for o in range(sea_groups):
            pl.semaphore_signal(barrier, inc=1, device_id={"grp": air_groups + o})
        for c in (l_asend, l_air, l_owner, l_counts, l_anbr, l_fw, l_amix, l_mw, l_sea):
            c.start()
        neighbours = anbr.shape[2]
        excess = row_count - columns
        tile = 256

        l_asend.wait()
        l_air.wait()
        packed(air_out, asend, apool)
        l_owner.wait()
        owners = [owner[0, 0, 0, b] for b in range(blocks)]
        slots = []
        for b in range(blocks):
            s = jnp.int32(b if same else 0)
            if not same:
                for e in range(b):
                    s = s + jnp.where(owners[e] == owners[b], 1, 0)
            slots.append(s)
        for b in range(blocks):
            codes_out[b : b + 1, :] = jnp.full((1, 128), owners[b] * capacity + slots[b], I32)
        if codes_out.shape[0] > blocks:
            codes_out[blocks:, :] = jnp.full((codes_out.shape[0] - blocks, 128), -1, I32)
        pl.semaphore_wait(barrier, 2 + sea_groups)
        sides = halos(levels_a)
        for c in sides:
            c.start()
        for o in range(sea_groups):
            code_copy(mine, o).start()

        l_counts.wait()
        column = row_columns(counts[...], row_count).astype(I32)
        low, high_of = column & (tile - 1), column >> (tile.bit_length() - 1)
        low_rows = as_rows(low, 16)

        def reach(p):
            first = max(0, p * tile - excess) // tile
            last = min(columns - 1, p * tile + tile - 1) // tile
            return range(first, last + 1)

        for p in range(row_count // tile):
            at = slice(p * tile, (p + 1) * tile)
            marks = [hot_rows(high_of[:, at], h, 16) for h in reach(p)]
            for t in range(tile // 16):
                part = low_hot(low_rows[:, at], t)
                for i, h in enumerate(reach(p)):
                    member[h * tile + t * 16 : h * tile + (t + 1) * 16, at] = part * marks[i]

        l_anbr.wait()
        base_a = base_of(amat.shape[0])

        def build(c, _):
            at = pl.ds(pl.multiple_of(c * width, width), width)
            rows_in = [anbr[0, 0, k : k + 1, at] for k in range(neighbours)]
            counts_matrix(amat, high, rows_in, base_a, at)
            return _

        lax.fori_loop(0, columns // width, build, 0)

        l_fw.wait()
        state = air_out[0, 0]
        top = state.astype(BF)
        weight = two_parts(fw[...])
        own = joined(mm(weight, top) + mm(weight, (state - top.astype(F32)).astype(BF)))
        gpool[:, :columns] = two_parts(own)
        take_halo(sides, apool, levels_a, columns)
        gpool[:, columns:] = two_parts(joined(mm(weight, apool[:, columns:])))
        l_amix.wait()
        l_mw.wait()
        for c in range(columns // tile):
            at = slice(c * tile, (c + 1) * tile)
            mean = joined(mm(gpool[...], amat[:, at])) * (1.0 / neighbours)
            here = own[:, at]
            slab[: 2 * fields, at] = two_parts(here + amix[0, :, at] * (mean - here))
        for p in range(row_count // tile):
            at = slice(p * tile, (p + 1) * tile)
            ks = reach(p)
            ks = slice(ks[0] * tile, (ks[-1] + 1) * tile)
            values = joined(mm(slab[: 2 * fields, ks], member[ks, at])) * mw[0, :, at]
            per = tile // block
            for q in range(per // 2):
                b = slice(2 * q * block, (2 * q + 1) * block), slice((2 * q + 1) * block, (2 * q + 2) * block)
                up_out[p * (per // 2) + q] = jnp.concatenate([values[:, b[0]], values[:, b[1]]], axis=0).astype(BF)
                up_copy(mine, p * (per // 2) + q).start()
        for c in range(columns // width):
            at = slice(c * width, (c + 1) * width)
            mean = mm(apool[...], amat[:, at]) * (1.0 / neighbours)
            here = air_out[0, 0, :, at]
            air_out[0, 0, :, at] = here + amix[0, :, at] * (mean - here)
        for o in range(sea_groups):
            down_copy(0, o).wait_recv()
        for b in range(blocks):
            at = slice(b * block, (b + 1) * block)
            share = jnp.broadcast_to(mw[0, :, at], (ret_pad, block))
            value = down_in[owners[b], slots[b]].astype(F32) * share
            slab[: 2 * ret_pad, at] = two_parts(value)
            slab[2 * ret_pad : 4 * ret_pad, at] = two_parts(share)
        for c in range(columns // tile):
            at = slice(c * tile, (c + 1) * tile)
            rs = slice(c * tile, min(row_count, (c + 1) * tile + excess))
            sums = lax.dot_general(slab[: 4 * ret_pad, rs], member[at, rs], NT, preferred_element_type=F32)
            ratio = joined(sums[: 2 * ret_pad]) / joined(sums[2 * ret_pad :])
            for f in range(ret_fields):
                back_out[0, f, :, at] = ratio[f : f + 1]
        for o in range(sea_groups):
            code_copy(mine, o).wait_send()
        for p in range(pairs):
            up_copy(mine, p).wait_send()
        l_sea.wait()

    @pl.when(jnp.logical_not(is_air))
    def _():
        for s in range(air_groups):
            pl.semaphore_signal(barrier, inc=1, device_id={"grp": s})
        not_first, not_last = mine > 0, mine < sea_groups - 1

        @pl.when(not_first)
        def _():
            pl.semaphore_signal(barrier, inc=1, device_id={"grp": g - 1})

        @pl.when(not_last)
        def _():
            pl.semaphore_signal(barrier, inc=1, device_id={"grp": g + 1})

        for c in (l_osend, l_sea, l_recv, l_retw, l_onbr, l_omix, l_force, l_air):
            c.start()
        l_osend.wait()
        l_sea.wait()
        packed(sea_out, osend, opool)
        links = jnp.where(not_first, 1, 0) + jnp.where(not_last, 1, 0)
        pl.semaphore_wait(barrier, 2 + air_groups + links)
        sides = halos(levels_o)
        for c in sides:
            c.start()
        neighbours = onbr.shape[1]
        l_retw.wait()
        retw[...] = jnp.zeros(retw.shape, F32)
        retw[:ret_fields] = retw_in[...]
        returned = jnp.dot(
            retw[...], sea_out[0, 0], precision=EXACT, preferred_element_type=F32).astype(BF)
        for h in range(highs):
            ret_bf[h * ret_pad : (h + 1) * ret_pad] = returned[:, h * base : (h + 1) * base]
        l_recv.wait()

        def slot_ids(s):
            return jnp.concatenate([recv[0, 0, k, s : s + 1, :] for k in range(capacity)], axis=1)

        for s in range(air_groups):
            idx = slot_ids(s)
            at = slice(s * span, (s + 1) * span)
            low = as_rows(idx & (base - 1), 16)
            for t in range(base // 16):
                lowmat[t * 16 : (t + 1) * 16, at] = low_hot(low, t)
            found = mm(ret_bf[...], lowmat[:, at])
            high_of = jnp.broadcast_to(idx >> bits, (ret_pad, span))
            looked = jnp.zeros((ret_pad, span), F32)
            for h in range(highs):
                looked = jnp.where(high_of == h, found[h * ret_pad : (h + 1) * ret_pad], looked)
            for k in range(capacity):
                down_out[s, k] = looked[:, k * block : (k + 1) * block].astype(BF)
            down_copy(s, mine).start()
        spread[...] = jnp.zeros(spread.shape, BF)
        wide_force[...] = jnp.zeros(wide_force.shape, F32)
        l_force.wait()
        strong = force[...]
        wide_force[:fields, :levels_o] = strong
        wide_force[field_pad : field_pad + fields, :levels_o] = strong
        wide_force[2 * field_pad : 2 * field_pad + fields, :levels_o] = strong - strong.astype(BF).astype(F32)
        force_rows = wide_force[...].T[:levels_o, : 3 * field_pad].astype(BF)
        l_onbr.wait()
        l_omix.wait()
        base_p = base_of(omat0.shape[0])
        tiles = cells // width

        def build(c, mat, marks):
            at = pl.ds(pl.multiple_of(c * width, width), width)
            rows_in = [onbr[0, k, :, at] for k in range(neighbours)]
            counts_matrix(mat, marks, rows_in, base_p, slice(0, width))

        def product(c, mat):
            at = pl.ds(pl.multiple_of(c * width, width), width)
            mean = mm(opool[...], mat[...]) * (1.0 / neighbours)
            here = sea_out[0, 0, :, at]
            sea_out[0, 0, :, at] = here + omix[0, :, at] * (mean - here)

        build(0, omat0, high)
        take_halo(sides, opool, levels_o, cells)

        def pair(i, _):
            product(2 * i, omat0)
            build(2 * i + 1, omat1, high1)
            product(2 * i + 1, omat1)
            build(2 * i + 2, omat0, high)
            return _

        lax.fori_loop(0, tiles // 2 - 1, pair, 0)
        product(tiles - 2, omat0)
        build(tiles - 1, omat1, high1)
        product(tiles - 1, omat1)
        row_span = blocks * block
        rows_low, rows_high = [], []
        for s in range(air_groups):
            code_copy(s, 0).wait_recv()
            place = codes_in[s] - mine * capacity
            ids = []
            for b in range(blocks):
                here = place[b : b + 1]
                held = (here >= 0) & (here < capacity)
                if same:
                    cell = recv[0, 0, b, s : s + 1, :]
                else:
                    cell = jnp.zeros((1, block), I32)
                    for k in range(capacity):
                        cell = jnp.where(here == k, recv[0, 0, k, s : s + 1, :], cell)
                ids.append(jnp.where(held, cell, -1))
            rows_high.append([i >> bits for i in ids])
            if not same:
                low = as_rows(jnp.concatenate(ids, axis=1) & (base - 1), 16)
                for t in range(base // 16):
                    lowrow[t * 16 : (t + 1) * 16, s * row_span : (s + 1) * row_span] = low_hot(low, t)
        near = lowmat if same else lowrow
        flux = jnp.zeros((highs * field_pad, base), F32)
        for p in range(pairs):
            for s in range(air_groups):
                relay_copy(s, p).wait_recv()

                @pl.when(not_last)
                def _():
                    relay_copy(s, p).start()

            for s in range(air_groups):
                arrived = up_in[s, p].astype(F32)
                for j in range(2):
                    at = slice(s * row_span + (2 * p + j) * block, s * row_span + (2 * p + j + 1) * block)
                    part = arrived[j * fields : (j + 1) * fields]
                    high_of = jnp.broadcast_to(rows_high[s][2 * p + j], (fields, block))
                    for h in range(highs):
                        spread[h * field_pad : h * field_pad + fields, at] = (
                            jnp.where(high_of == h, part, 0.0).astype(BF))
                at = slice(s * row_span + 2 * p * block, s * row_span + (2 * p + 2) * block)
                flux = flux + lax.dot_general(spread[:, at], near[:, at], NT, preferred_element_type=F32)
        for h in range(highs):
            at = slice(h * base, (h + 1) * base)
            here = flux[h * field_pad : (h + 1) * field_pad]
            top = here.astype(BF)
            rest = (here - top.astype(F32)).astype(BF)
            sea_out[0, 0, :, at] += mm(force_rows, jnp.concatenate([top, rest, top], axis=0))
        for s in range(air_groups):
            down_copy(s, mine).wait_send()

        @pl.when(not_last)
        def _():
            for p in range(pairs):
                for s in range(air_groups):
                    relay_copy(s, p).wait_send()

        back_out[...] = jnp.zeros(back_out.shape, F32)
        l_air.wait()


def finish(a, b, c, a_out, b_out, c_out, sem):
    copies = [
        pltpu.make_async_copy(x, y, sem.at[i])
        for i, (x, y) in enumerate(((a, a_out), (b, b_out), (c, c_out)))
    ]
    for x in copies:
        x.start()
    for x in copies:
        x.wait()


def solution(mesh):
    groups, devs = mesh.shape["grp"], mesh.shape["dev"]
    in_specs = (
        P("grp", "dev", None, None), P("grp", "dev", None, None), P("grp", "dev", None),
        P("grp", "dev", None), P(), P("grp", "dev", None), P("grp", "dev", None),
        P("grp", "dev", None, None), P("grp", "dev", None, None, None),
        P("grp", "dev", None, None), P("grp", "dev", None, None), P("grp", "dev", None),
        P("grp", "dev", None), P(), P(),
    )
    out_specs = (P("grp", "dev", None, None),) * 3

    def on_device(*args):
        args = list(args)
        args[5] = args[5].reshape(-1, 128)
        args[7] = args[7].transpose(0, 1, 3, 2)
        args[8] = args[8].transpose(0, 1, 3, 2, 4)
        args[10] = args[10].transpose(0, 2, 1, 3)
        args[13] = args[13].T
        air, anbr, asend, amix, fw, counts, mw, owner, recv, sea, onbr, osend, omix, force, ret = args
        levels_a, columns = air.shape[2:]
        levels_o, cells = sea.shape[2:]
        half = asend.shape[2] // 2
        capacity, air_groups, block = recv.shape[2:]
        sea_groups = groups - air_groups
        blocks = owner.shape[3]
        fields, ret_fields = fw.shape[0], ret.shape[0]
        ret_pad = -(-ret_fields // 16) * 16
        field_pad = -(-fields // 16) * 16
        row_count = mw.shape[2]
        pairs = blocks // 2
        pool_a, pool_o = columns + 2 * half, cells + 2 * half
        width = 256
        base, span = base_of(cells), air_groups * capacity * block
        row_span = air_groups * blocks * block
        same = capacity == blocks
        deep = max(
            anbr.shape[2] * (pool_a // base_of(pool_a)),
            onbr.shape[1] * (pool_o // base_of(pool_o)),
        )
        code_rows = -(-blocks // 8) * 8
        V = pltpu.VMEM
        dma = pltpu.SemaphoreType.DMA
        kept = [V(x.shape, x.dtype) for x in (anbr, asend, amix, fw, counts, mw)]
        kept += [pltpu.SMEM(owner.shape, owner.dtype)]
        kept += [V(x.shape, x.dtype) for x in (recv, onbr, osend, omix, force, ret)]
        scratch = kept + [
            V((2, max(levels_a, levels_o), half), BF), V((2, max(levels_a, levels_o), half), BF),
            V((levels_a, pool_a), BF), V((2 * fields, pool_a), BF), V((levels_o, pool_o), BF),
            V((pool_a, columns), BF), V((pool_o, width), BF), V((pool_o, width), BF),
            V((columns, row_count), BF), V((base, span), BF),
            V((base if not same else 16, row_span if not same else 128), BF),
            V((cells // base * field_pad, row_span), BF),
            V((deep, 16, width), BF), V((deep, 16, width), BF),
            V((code_rows, 128), I32), V((air_groups, code_rows, 128), I32),
            V((pairs, 2 * fields, block), BF), V((air_groups, pairs, 2 * fields, block), BF),
            V((air_groups, capacity, ret_pad, block), BF), V((sea_groups, capacity, ret_pad, block), BF),
            V((ret_pad, levels_o), F32),
            V((max(4 * ret_pad, 2 * fields), max(row_count, columns)), BF),
            V((cells // base * ret_pad, base), BF),
            V((128, 128), F32),
            dma((15,)), dma((2,)), dma((2,)), dma((sea_groups,)), dma((air_groups,)),
            dma((pairs,)), dma((air_groups, pairs)), dma((air_groups, pairs)),
            dma((air_groups,)), dma((sea_groups,)),
        ]
        vmem = pl.BlockSpec(memory_space=pltpu.VMEM)
        outs = (
            jax.ShapeDtypeStruct(air.shape, F32),
            jax.ShapeDtypeStruct(sea.shape, F32),
            jax.ShapeDtypeStruct((1, ret_fields, 1, columns), F32),
        )
        parts = pl.pallas_call(
            functools.partial(kernel, (groups, devs, air_groups)),
            out_shape=outs,
            in_specs=[pl.BlockSpec(memory_space=pltpu.HBM)] * 15,
            out_specs=(vmem,) * 3,
            scratch_shapes=scratch,
            compiler_params=pltpu.CompilerParams(
                collective_id=0, has_side_effects=True, vmem_limit_bytes=48 * 1024 * 1024),
            name="couple",
        )(*[pltpu.with_memory_space_constraint(x, pltpu.HBM) for x in args])
        air_next, sea_next, back = pl.pallas_call(
            finish,
            out_shape=outs,
            in_specs=[pl.BlockSpec(memory_space=pl.ANY)] * 3,
            out_specs=(pl.BlockSpec(memory_space=pl.ANY),) * 3,
            scratch_shapes=[dma((3,))],
            compiler_params=pltpu.CompilerParams(vmem_limit_bytes=1024 * 1024),
            name="finish",
        )(*parts)
        return air_next, sea_next, back.transpose(0, 2, 1, 3)

    return jax.shard_map(
        on_device, mesh=mesh, in_specs=in_specs, out_specs=out_specs, check_vma=False)
```

profile of v0, /device:TPU:24, one launch (start us, length us, event | category | flops | bytes accessed | tf_op | source)
XLA Modules:
  0.0 17.6 jit_solution(13372805869100997515)
XLA Ops:
  0.6 15.9 %couple.1 = (f32[1,1,128,1024]{3,2,1,0:T(8,128)S(1)}, f32[1,1,80,2048]{3,2,1,0:T(8,128)S(1)}, f32[1,12,1,1024]{3,2,1,0:T(1,128)S(1)}) custom-call(f32[1,1,128,1024]{3,2,1,0:T(8,128)} %air_hbm.1, s32[1,1,4,1024]{3,2,1,0:T(4,128)} %anbr_hbm.1, s32[1,1,256]{2,1,0:T(1,128)} %asend_hbm.1, f32[1,1,1024]{2,1,0:T(1,128)} %amix_hbm.1, f32[24,128]{1,0:T(8,128)} %fw_hbm.1, ...), custom_call_target="tpu_custom_call" | custom-call | tf_op jit(solution)/shard_map/couple/pallas_call | solution.py:537
  16.6 1.0 %finish.1 = (f32[1,1,128,1024]{3,2,1,0:T(8,128)}, f32[1,1,80,2048]{3,2,1,0:T(8,128)}, f32[1,12,1,1024]{3,2,1,0:T(1,128)}) custom-call(f32[1,1,128,1024]{3,2,1,0:T(8,128)S(1)} %get-tuple-element.9.a, f32[1,1,80,2048]{3,2,1,0:T(8,128)S(1)} %get-tuple-element.10.b, f32[1,12,1,1024]{3,2,1,0:T(1,128)S(1)} %get-tuple-element.11.c), custom_call_target="tpu_custom_call" | custom-call | tf_op jit(solution)/shard_map/finish/pallas_call | solution.py:547
where the time goes:
time: 17.9 us; the launch traced here: 17.6 us
  Pallas kernels  17 us (95%)
  between operations  0.64 us (4%)
    pallas_call x1, Pallas kernels, on_device(): pl.pallas_call(functools.partial(kernel, (groups, devs, air_groups)), out...  15.9 us
    pallas_call x1, Pallas kernels, on_device(): pl.pallas_call(finish, out_shape=outs, in_specs=[pl.BlockSpec(memory_spac...  1.04 us

commit v1 on v0

v1 whole, which is shorter than its diff:
```python
import functools

import jax
import jax.numpy as jnp
from jax import lax
from jax.experimental import pallas as pl
from jax.experimental.pallas import tpu as pltpu
from jax.sharding import PartitionSpec as P

EXACT = lax.Precision.HIGHEST
BF = jnp.bfloat16
F32 = jnp.float32
I32 = jnp.int32
NT = (((1,), (1,)), ((), ()))
TN = (((0,), (0,)), ((), ()))


def mm(a, b):
    return jnp.dot(a, b, preferred_element_type=F32)


def two_parts(x):
    rest = x - x.astype(BF).astype(F32)
    return jnp.concatenate([x, rest], axis=0).astype(BF)


def joined(x):
    half = x.shape[0] // 2
    return x[:half] + x[half:]


def low_hot(low, t):
    place = lax.broadcasted_iota(I32, low.shape, 0).astype(F32) + 16.0 * t
    return jnp.where(low == place.astype(BF), jnp.asarray(1, BF), jnp.asarray(0, BF))


def as_rows(idx, rows):
    return jnp.broadcast_to(idx.astype(F32), (rows, idx.shape[1])).astype(BF)


def hot_rows(high, h, rows):
    return jnp.where(as_rows(high, rows) == jnp.asarray(h, BF), jnp.asarray(1, BF), jnp.asarray(0, BF))


def one_hot_matrix(out_ref, idx, base):
    bits = base.bit_length() - 1
    low = as_rows(idx & (base - 1), 16)
    marks = [hot_rows(idx >> bits, h, 16) for h in range(out_ref.shape[0] // base)]
    for t in range(base // 16):
        part = low_hot(low, t)
        for h, mark in enumerate(marks):
            out_ref[h * base + t * 16 : h * base + (t + 1) * 16, :] = part * mark


def couples(highs, neighbours):
    step = 2 if neighbours < 8 else 1
    return [tuple(range(h, min(h + step, highs))) for h in range(0, highs, step)]


def scale_at(position, length, base, neighbours):
    for couple in couples(length // base, neighbours):
        if position // base in couple:
            return 16.0 if len(couple) == 2 and position // base == couple[0] else 1.0


def scaled(x, at, length, base, neighbours):
    return x * jnp.asarray(scale_at(at, length, base, neighbours), BF)


def counts_matrix(out_ref, high_ref, idx_rows, base, at):
    highs = out_ref.shape[0] // base
    bits = base.bit_length() - 1
    lines = couples(highs, len(idx_rows))
    low = [as_rows(i & (base - 1), 16) for i in idx_rows]
    for k, i in enumerate(idx_rows):
        top = as_rows(i >> bits, 16)
        for n, couple in enumerate(lines):
            mark = jnp.where(top == jnp.asarray(couple[-1], BF), jnp.asarray(1, BF), jnp.asarray(0, BF))
            if len(couple) == 2:
                mark = jnp.where(top == jnp.asarray(couple[0], BF), jnp.asarray(1 / 16, BF), mark)
            high_ref[k * len(lines) + n] = mark
    for t in range(base // 16):
        parts = [low_hot(i, t) for i in low]
        for n, couple in enumerate(lines):
            total = parts[0] * high_ref[n]
            for k in range(1, len(parts)):
                total = total + parts[k] * high_ref[k * len(lines) + n]
            if len(couple) == 2:
                whole = (total + jnp.asarray(128, BF)) - jnp.asarray(128, BF)
                out_ref[couple[0] * base + t * 16 : couple[0] * base + (t + 1) * 16, at] = total - whole
                total = whole
            out_ref[couple[-1] * base + t * 16 : couple[-1] * base + (t + 1) * 16, at] = total


def base_of(length):
    return 256 if length % 256 == 0 else 128


def row_columns(counts, rows):
    lines = counts.shape[0]
    wide = jnp.concatenate([counts.astype(F32), jnp.zeros((-lines % 16, 128), F32)], axis=0).astype(BF)
    lines = wide.shape[0]
    i = lax.broadcasted_iota(I32, (128, 128), 0)
    j = lax.broadcasted_iota(I32, (128, 128), 1)
    within = mm(wide, jnp.where(i <= j, 1.0, 0.0).astype(BF))
    i = lax.broadcasted_iota(I32, (lines, lines), 0)
    j = lax.broadcasted_iota(I32, (lines, lines), 1)
    ones = jnp.ones((128, 128), BF)
    before = mm(mm(jnp.where(j < i, 1.0, 0.0).astype(BF), wide).astype(BF), ones)
    upto = mm(mm(jnp.where(j <= i, 1.0, 0.0).astype(BF), wide).astype(BF), ones)
    offsets = within + before
    high = jnp.floor(offsets * (1.0 / 256.0)) * 256.0
    halves = jnp.concatenate([high, offsets - high], axis=0).astype(BF)
    tiles = rows // 128
    at = lax.broadcasted_iota(I32, (lines, rows), 1).astype(F32)
    ends = jnp.concatenate([upto] * tiles, axis=1)
    starts = jnp.concatenate([before] * tiles, axis=1)
    passed = jnp.where(ends <= at, 1.0, 0.0)
    line = jnp.where(starts <= at, 1.0, 0.0) - passed
    line = jnp.concatenate([line, line], axis=0).astype(BF)
    ends_in = lax.dot_general(halves, line, TN, preferred_element_type=F32)
    at = lax.broadcasted_iota(I32, (128, rows), 1).astype(F32)
    inner = jnp.sum(jnp.where(ends_in <= at, 1.0, 0.0), axis=0, keepdims=True)
    return 128.0 * jnp.sum(passed, axis=0, keepdims=True) + inner


def kernel(sizes, *refs):
    pl.run_scoped(
        functools.partial(body, sizes[:3], refs),
        *(pltpu.SemaphoreType.DMA(n) for n in sizes[3]))


def body(
    sizes, refs, load, halo_send, x_send, up_send,
):
    (
        air_hbm, anbr_hbm, asend_hbm, amix_hbm, fw_hbm, counts_hbm, mw_hbm, owner_hbm,
        recv_hbm, sea_hbm, onbr_hbm, osend_hbm, omix_hbm, force_hbm, retw_hbm,
        air_out, sea_out, back_out, flux_out, force_out,
        anbr, asend, amix, fw, counts, mw, owner, recv, onbr, osend, omix, force, retw_in,
        pack, halo, gpack, ghalo, apool, gpool, opool, picker, amat, omat, member, ahead, early, lowmat, lowrow, spread, high,
        codes_out, codes_in, up_out, up_in, down_out, down_in, retw, slab, ret_bf, wide_force,
        halo_recv, x_recv, up_recv,
    ) = refs
    groups, devs, air_groups = sizes
    sea_groups = groups - air_groups
    g, d = lax.axis_index("grp"), lax.axis_index("dev")
    lower, upper = lax.rem(d + devs - 1, devs), lax.rem(d + 1, devs)
    is_air = g < air_groups
    mine = jnp.where(is_air, g, g - air_groups)
    half = halo.shape[2]
    capacity, block = recv.shape[2], recv.shape[4]
    span = capacity * block
    levels_a, columns = air_out.shape[2:]
    levels_o, cells = sea_out.shape[2:]
    fields = fw.shape[0]
    ret_fields = retw_in.shape[0]
    ret_pad = retw.shape[0]
    blocks = owner.shape[3]
    row_count = mw.shape[2]
    pairs = blocks // 2
    same = capacity == blocks
    base = lowmat.shape[0]
    bits = base.bit_length() - 1
    highs = cells // base
    field_pad = spread.shape[0] // highs
    width = high.shape[2]

    barrier = pltpu.get_barrier_semaphore()
    pl.semaphore_signal(barrier, inc=1, device_id={"dev": lower})
    pl.semaphore_signal(barrier, inc=1, device_id={"dev": upper})

    def loads(*copies):
        return [pltpu.make_async_copy(a, b, load.at[i]) for i, (a, b) in enumerate(copies)]

    def halos(source, target, levels, first):
        return [
            pltpu.make_async_remote_copy(
                src_ref=source.at[1 - side, :levels], dst_ref=target.at[side, :levels],
                send_sem=halo_send.at[first + side], recv_sem=halo_recv.at[first + side],
                device_id={"dev": upper if side == 0 else lower})
            for side in range(2)
        ]

    def code_copy(s, o):
        return pltpu.make_async_remote_copy(
            src_ref=codes_out, dst_ref=codes_in.at[s], send_sem=x_send.at[o],
            recv_sem=x_recv.at[s], device_id={"grp": air_groups + o})

    def down_copy(s, o):
        return pltpu.make_async_remote_copy(
            src_ref=down_out.at[s], dst_ref=down_in.at[o], send_sem=x_send.at[s],
            recv_sem=x_recv.at[o], device_id={"grp": s})

    def up_copy(s, p):
        return pltpu.make_async_remote_copy(
            src_ref=up_out.at[p], dst_ref=up_in.at[s, p], send_sem=up_send.at[0, p],
            recv_sem=up_recv.at[s, p], device_id={"grp": air_groups})

    def relay_copy(s, p):
        return pltpu.make_async_remote_copy(
            src_ref=up_in.at[s, p], dst_ref=up_in.at[s, p], send_sem=up_send.at[s, p],
            recv_sem=up_recv.at[s, p], device_id={"grp": g + 1})

    def packed(chosen, to, levels):
        to[0, :levels, :] = chosen[:, :half]
        to[1, :levels, :] = chosen[:, half:]

    def take_halo(copies, pool, levels, length, neighbours):
        for c in copies:
            c.wait()
        for side in range(2):
            at = slice(length + side * half, length + (side + 1) * half)
            pool[:, at] = scaled(halo[side, :levels, :], at.start, pool.shape[1], base_of(pool.shape[1]), neighbours)

    @pl.when(is_air)
    def _():
        for o in range(sea_groups):
            pl.semaphore_signal(barrier, inc=1, device_id={"grp": air_groups + o})
        (l_asend, l_air, l_fw, l_owner, l_counts, l_anbr, l_amix, l_mw, l_sea) = loads(
            (asend_hbm, asend), (air_hbm, air_out), (fw_hbm, fw), (owner_hbm, owner), (counts_hbm, counts),
            (anbr_hbm, anbr), (amix_hbm, amix), (mw_hbm, mw), (sea_hbm, sea_out))
        for c in (l_asend, l_fw, l_air, l_owner, l_counts, l_anbr, l_amix, l_mw):
            c.start()
        neighbours = anbr.shape[2]
        excess = row_count - columns
        tile = 256

        l_asend.wait()
        base_a = base_of(amat.shape[0])
        one_hot_matrix(picker.at[:columns], asend[0], base_of(columns))
        l_fw.wait()
        weight = two_parts(fw[...])
        l_air.wait()
        state = air_out[0, 0]
        top = state.astype(BF)
        own = joined(mm(weight, top) + mm(weight, (state - top.astype(F32)).astype(BF)))
        own_parts = two_parts(own)
        packed(mm(own_parts, picker[:columns]).astype(BF), gpack, 2 * fields)
        pl.semaphore_wait(barrier, 2 + sea_groups)
        near_sides = halos(gpack, ghalo, 2 * fields, 2)
        for c in near_sides:
            c.start()
        packed(mm(top, picker[:columns]).astype(BF), pack, levels_a)
        for h in range(columns // base_a):
            at = slice(h * base_a, (h + 1) * base_a)
            apool[:, at] = scaled(top[:, at], at.start, amat.shape[0], base_a, neighbours)
            gpool[:, at] = scaled(own_parts[:, at], at.start, amat.shape[0], base_a, neighbours)
        sides = halos(pack, halo, levels_a, 0)
        for c in sides:
            c.start()
        l_owner.wait()
        owners = [owner[0, 0, 0, b] for b in range(blocks)]
        slots = []
        for b in range(blocks):
            s = jnp.int32(b if same else 0)
            if not same:
                for e in range(b):
                    s = s + jnp.where(owners[e] == owners[b], 1, 0)
            slots.append(s)
        for b in range(blocks):
            codes_out[b : b + 1, :] = jnp.full((1, 128), owners[b] * capacity + slots[b], I32)
        if codes_out.shape[0] > blocks:
            codes_out[blocks:, :] = jnp.full((codes_out.shape[0] - blocks, 128), -1, I32)
        for o in range(sea_groups):
            code_copy(mine, o).start()
        l_sea.start()

        l_counts.wait()
        l_anbr.wait()
        l_amix.wait()
        l_mw.wait()
        column = row_columns(counts[...], row_count).astype(I32)
        low, high_of = column & (tile - 1), column >> (tile.bit_length() - 1)
        low_rows = as_rows(low, 16)

        def reach(p):
            first = max(0, p * tile - excess) // tile
            last = min(columns - 1, p * tile + tile - 1) // tile
            return range(first, last + 1)

        for p in range(row_count // tile):
            at = slice(p * tile, (p + 1) * tile)
            marks = [hot_rows(high_of[:, at], h, 16) for h in reach(p)]
            for t in range(tile // 16):
                part = low_hot(low_rows[:, at], t)
                for i, h in enumerate(reach(p)):
                    member[h * tile + t * 16 : h * tile + (t + 1) * 16, at] = part * marks[i]

        for c in range(columns // width):
            at = slice(c * width, (c + 1) * width)
            counts_matrix(amat, high, [anbr[0, 0, k : k + 1, at] for k in range(neighbours)], base_a, at)
        for c in range(columns // tile):
            at = slice(c * tile, (c + 1) * tile)
            mean = joined(mm(gpool[...], amat[:columns, at])) * (1.0 / neighbours)
            here, mix = own[:, at], amix[0, :, at]
            flux = here + mix * (mean - here)
            slab[: 2 * fields, at] = two_parts(flux)
            slab[2 * fields : 2 * fields + 16, at] = two_parts(jnp.broadcast_to(mix, (8, tile)))
        for p in range(row_count // tile):
            at = slice(p * tile, (p + 1) * tile)
            ks = reach(p)
            ks = slice(ks[0] * tile, (ks[-1] + 1) * tile)
            both = mm(slab[: 2 * fields + 16, ks], member[ks, at])
            share = mw[0, :, at]
            mix = joined(both[2 * fields :])[:1]
            early[:fields, at] = joined(both[: 2 * fields]) * share
            early[fields : fields + 8, at] = jnp.broadcast_to(share * mix * (1.0 / neighbours), (8, tile))
            ahead[:, at] = mm(amat[columns:, ks], member[ks, at]).astype(BF)
        for c in near_sides:
            c.wait()
        far = jnp.concatenate([
            scaled(ghalo[side], columns + side * half, amat.shape[0], base_a, neighbours) for side in range(2)], axis=1)
        for p in range(row_count // tile):
            at = slice(p * tile, (p + 1) * tile)
            values = early[:fields, at] + early[fields : fields + 1, at] * joined(mm(far, ahead[:, at]))
            per = tile // block
            for q in range(per // 2):
                b = slice(2 * q * block, (2 * q + 1) * block), slice((2 * q + 1) * block, (2 * q + 2) * block)
                up_out[p * (per // 2) + q] = jnp.concatenate([values[:, b[0]], values[:, b[1]]], axis=0).astype(BF)
                up_copy(mine, p * (per // 2) + q).start()
        take_halo(sides, apool, levels_a, columns, neighbours)
        for c in range(columns // width):
            at = slice(c * width, (c + 1) * width)
            mean = mm(apool[...], amat[:, at]) * (1.0 / neighbours)
            here = air_out[0, 0, :, at]
            air_out[0, 0, :, at] = here + amix[0, :, at] * (mean - here)
        for o in range(sea_groups):
            down_copy(0, o).wait_recv()
        for b in range(blocks):
            at = slice(b * block, (b + 1) * block)
            share = jnp.broadcast_to(mw[0, :, at], (ret_pad, block))
            value = down_in[owners[b], slots[b]].astype(F32) * share
            slab[: 2 * ret_pad, at] = two_parts(value)
            slab[2 * ret_pad : 4 * ret_pad, at] = two_parts(share)
        for c in range(columns // tile):
            at = slice(c * tile, (c + 1) * tile)
            rs = slice(c * tile, min(row_count, (c + 1) * tile + excess))
            sums = lax.dot_general(slab[: 4 * ret_pad, rs], member[at, rs], NT, preferred_element_type=F32)
            ratio = joined(sums[: 2 * ret_pad]) / joined(sums[2 * ret_pad :])
            for f in range(ret_fields):
                back_out[0, f, :, at] = ratio[f : f + 1]
        for o in range(sea_groups):
            code_copy(mine, o).wait_send()
        for p in range(pairs):
            up_copy(mine, p).wait_send()
        l_sea.wait()

    @pl.when(jnp.logical_not(is_air))
    def _():
        for s in range(air_groups):
            pl.semaphore_signal(barrier, inc=1, device_id={"grp": s})
        not_first, not_last = mine > 0, mine < sea_groups - 1

        @pl.when(not_first)
        def _():
            pl.semaphore_signal(barrier, inc=1, device_id={"grp": g - 1})

        @pl.when(not_last)
        def _():
            pl.semaphore_signal(barrier, inc=1, device_id={"grp": g + 1})

        (l_osend, l_sea, l_retw, l_recv, l_onbr, l_omix, l_force, l_air) = loads(
            (osend_hbm, osend), (sea_hbm, sea_out), (retw_hbm, retw_in), (recv_hbm, recv), (onbr_hbm, onbr),
            (omix_hbm, omix), (force_hbm, force), (air_hbm, air_out))
        for c in (l_osend, l_sea, l_retw, l_recv, l_onbr, l_omix, l_force):
            c.start()
        neighbours = onbr.shape[1]
        l_osend.wait()
        one_hot_matrix(picker.at[:cells], osend[0], base)
        base_p = base_of(omat.shape[0])
        l_sea.wait()
        top = sea_out[0, 0].astype(BF)
        packed(mm(top, picker[:cells]).astype(BF), pack, levels_o)
        links = jnp.where(not_first, 1, 0) + jnp.where(not_last, 1, 0)
        pl.semaphore_wait(barrier, 2 + air_groups + links)
        sides = halos(pack, halo, levels_o, 0)
        for c in sides:
            c.start()
        l_air.start()
        l_retw.wait()
        l_recv.wait()
        l_onbr.wait()
        l_omix.wait()
        l_force.wait()
        retw[...] = jnp.zeros(retw.shape, F32)
        retw[:ret_fields] = retw_in[...]
        weight = two_parts(retw[...])
        state = sea_out[0, 0]
        top = state.astype(BF)
        rest = (state - top.astype(F32)).astype(BF)
        for h in range(cells // base_p):
            at = slice(h * base_p, (h + 1) * base_p)
            opool[:, at] = scaled(top[:, at], at.start, omat.shape[0], base_p, neighbours)
        returned = joined(mm(weight, top) + mm(weight, rest)).astype(BF)
        for h in range(highs):
            ret_bf[h * ret_pad : (h + 1) * ret_pad] = returned[:, h * base : (h + 1) * base]

        def slot_ids(s):
            return jnp.concatenate([recv[0, 0, k, s : s + 1, :] for k in range(capacity)], axis=1)

        for s in range(air_groups):
            idx = slot_ids(s)
            at = slice(s * span, (s + 1) * span)
            low = as_rows(idx & (base - 1), 16)
            for t in range(base // 16):
                lowmat[t * 16 : (t + 1) * 16, at] = low_hot(low, t)
            found = mm(ret_bf[...], lowmat[:, at])
            high_of = jnp.broadcast_to(idx >> bits, (ret_pad, span))
            looked = jnp.zeros((ret_pad, span), F32)
            for h in range(highs):
                looked = jnp.where(high_of == h, found[h * ret_pad : (h + 1) * ret_pad], looked)
            for k in range(capacity):
                down_out[s, k] = looked[:, k * block : (k + 1) * block].astype(BF)
            down_copy(s, mine).start()
        wide_force[...] = jnp.zeros(wide_force.shape, F32)
        strong = force[...]
        wide_force[:fields, :levels_o] = strong
        wide_force[field_pad : field_pad + fields, :levels_o] = strong
        wide_force[2 * field_pad : 2 * field_pad + fields, :levels_o] = strong - strong.astype(BF).astype(F32)
        force_out[...] = wide_force[...].T.astype(BF)
        flux_out[...] = jnp.zeros(flux_out.shape, F32)
        back_out[...] = jnp.zeros(back_out.shape, F32)
        tiles = cells // width
        row_span = blocks * block
        near = lowmat if same else lowrow

        def build(c):
            at = slice(c * width, (c + 1) * width)
            counts_matrix(omat, high, [onbr[0, k, :, at] for k in range(neighbours)], base_p, at)

        def product(c, depth):
            at = slice(c * width, (c + 1) * width)
            mean = mm(opool[:, :depth], omat[:depth, at]) * (1.0 / neighbours)
            here = sea_out[0, 0, :, at]
            sea_out[0, 0, :, at] = here + omix[0, :, at] * (mean - here)

        def rim(c):
            at = slice(c * width, (c + 1) * width)
            mean = mm(opool[:, cells:], omat[cells:, at]) * (1.0 / neighbours)
            sea_out[0, 0, :, at] += omix[0, :, at] * mean

        def relay(p):
            for s in range(air_groups):
                relay_copy(s, p).wait_recv()

                @pl.when(not_last)
                def _():
                    relay_copy(s, p).start()

        rows_high = []

        def code():
            for s in range(air_groups):
                code_copy(s, 0).wait_recv()
                place = codes_in[s] - mine * capacity
                ids = []
                for b in range(blocks):
                    here = place[b : b + 1]
                    held = (here >= 0) & (here < capacity)
                    if same:
                        cell = recv[0, 0, b, s : s + 1, :]
                    else:
                        cell = jnp.zeros((1, block), I32)
                        for k in range(capacity):
                            cell = jnp.where(here == k, recv[0, 0, k, s : s + 1, :], cell)
                    ids.append(jnp.where(held, cell, -1))
                rows_high.append([i >> bits for i in ids])
                if not same:
                    low = as_rows(jnp.concatenate(ids, axis=1) & (base - 1), 16)
                    for t in range(base // 16):
                        lowrow[t * 16 : (t + 1) * 16, s * row_span : (s + 1) * row_span] = low_hot(low, t)

        def collect(p):
            total = flux_out[...]
            for s in range(air_groups):
                arrived = up_in[s, p].astype(F32)
                for j in range(2):
                    at = slice(s * row_span + (2 * p + j) * block, s * row_span + (2 * p + j + 1) * block)
                    part = jnp.concatenate(
                        [arrived[j * fields : (j + 1) * fields], jnp.zeros((field_pad - fields, block), F32)], axis=0)
                    high_of = jnp.broadcast_to(rows_high[s][2 * p + j], (field_pad, block))
                    for h in range(highs):
                        spread[h * field_pad : (h + 1) * field_pad, at] = (
                            jnp.where(high_of == h, part, 0.0).astype(BF))
                at = slice(s * row_span + 2 * p * block, s * row_span + (2 * p + 2) * block)
                total = total + lax.dot_general(spread[:, at], near[:, at], NT, preferred_element_type=F32)
            flux_out[...] = total

        build(0)
        late = min(5, tiles)
        for c in range(late):
            product(c, cells)
            if c + 1 < tiles:
                build(c + 1)
        take_halo(sides, opool, levels_o, cells, neighbours)
        for c in range(late):
            rim(c)
        for c in range(late, tiles):
            product(c, omat.shape[0])
            if c + 1 < tiles:
                build(c + 1)
        code()
        relay(0)
        for p in range(pairs):
            if p:
                relay(p)
            collect(p)
        for s in range(air_groups):
            down_copy(s, mine).wait_send()

        @pl.when(not_last)
        def _():
            for p in range(pairs):
                for s in range(air_groups):
                    relay_copy(s, p).wait_send()

        l_air.wait()


def finish(air_groups, a, b, c, flux, force, a_out, b_out, c_out, held, sem):
    is_air = lax.axis_index("grp") < air_groups
    base, field_pad = flux.shape[1], force.shape[1] // 4
    highs = flux.shape[0] // field_pad
    levels = b.shape[2]
    first = pltpu.make_async_copy(a, a_out, sem.at[0])
    last = pltpu.make_async_copy(c, c_out, sem.at[1])
    first.start()
    last.start()

    @pl.when(is_air)
    def _():
        whole = pltpu.make_async_copy(b, b_out, sem.at[2])
        whole.start()
        whole.wait()

    @pl.when(jnp.logical_not(is_air))
    def _():
        copies = []
        steps = 4 if highs % 4 == 0 else 1
        for i in range(steps):
            for h in range(i * highs // steps, (i + 1) * highs // steps):
                at = slice(h * base, (h + 1) * base)
                here = flux[h * field_pad : (h + 1) * field_pad]
                top = here.astype(BF)
                rest = (here - top.astype(F32)).astype(BF)
                three = jnp.concatenate([top, rest, top], axis=0)
                held[0, 0, :, at] = b[0, 0, :, at] + mm(force[:levels, : 3 * field_pad], three)
            at = slice(i * highs // steps * base, (i + 1) * highs // steps * base)
            copies.append(pltpu.make_async_copy(held.at[0, 0, :, at], b_out.at[0, 0, :, at], sem.at[2 + i]))
            copies[-1].start()
        for x in copies:
            x.wait()

    first.wait()
    last.wait()


def solution(mesh):
    groups, devs = mesh.shape["grp"], mesh.shape["dev"]
    in_specs = (
        P("grp", "dev", None, None), P("grp", "dev", None, None), P("grp", "dev", None),
        P("grp", "dev", None), P(), P("grp", "dev", None), P("grp", "dev", None),
        P("grp", "dev", None, None), P("grp", "dev", None, None, None),
        P("grp", "dev", None, None), P("grp", "dev", None, None), P("grp", "dev", None),
        P("grp", "dev", None), P(), P(),
    )
    out_specs = (P("grp", "dev", None, None),) * 3

    def on_device(*args):
        args = list(args)
        args[5] = args[5].reshape(-1, 128)
        args[7] = args[7].transpose(0, 1, 3, 2)
        args[8] = args[8].transpose(0, 1, 3, 2, 4)
        args[10] = args[10].transpose(0, 2, 1, 3)
        args[13] = args[13].T
        air, anbr, asend, amix, fw, counts, mw, owner, recv, sea, onbr, osend, omix, force, ret = args
        levels_a, columns = air.shape[2:]
        levels_o, cells = sea.shape[2:]
        half = asend.shape[2] // 2
        capacity, air_groups, block = recv.shape[2:]
        sea_groups = groups - air_groups
        blocks = owner.shape[3]
        fields, ret_fields = fw.shape[0], ret.shape[0]
        ret_pad = -(-ret_fields // 16) * 16
        field_pad = -(-fields // 16) * 16
        row_count = mw.shape[2]
        pairs = blocks // 2
        pool_a, pool_o = columns + 2 * half, cells + 2 * half
        width = 256
        base, span = base_of(cells), air_groups * capacity * block
        row_span = air_groups * blocks * block
        same = capacity == blocks
        deep = max(
            anbr.shape[2] * (pool_a // base_of(pool_a)),
            onbr.shape[1] * (pool_o // base_of(pool_o)),
        )
        code_rows = -(-blocks // 8) * 8
        V = pltpu.VMEM
        dma = pltpu.SemaphoreType.DMA
        kept = [V(x.shape, x.dtype) for x in (anbr, asend, amix, fw, counts, mw)]
        kept += [pltpu.SMEM(owner.shape, owner.dtype)]
        kept += [V(x.shape, x.dtype) for x in (recv, onbr, osend, omix, force, ret)]
        levels = max(levels_a, levels_o)
        scratch = kept + [
            V((2, levels, half), BF), V((2, levels, half), BF),
            V((2, 2 * fields, half), BF), V((2, 2 * fields, half), BF),
            V((levels_a, pool_a), BF), V((2 * fields, columns), BF), V((levels_o, pool_o), BF), V((max(columns, cells), 2 * half), BF),
            V((pool_a, columns), BF), V((pool_o, cells), BF),
            V((columns, row_count), BF), V((2 * half, row_count), BF), V((fields + 8, row_count), F32),
            V((base, span), BF),
            V((base if not same else 16, row_span if not same else 128), BF),
            V((cells // base * field_pad, row_span), BF),
            V((deep, 16, width), BF),
            V((code_rows, 128), I32), V((air_groups, code_rows, 128), I32),
            V((pairs, 2 * fields, block), BF), V((air_groups, pairs, 2 * fields, block), BF),
            V((air_groups, capacity, ret_pad, block), BF), V((sea_groups, capacity, ret_pad, block), BF),
            V((ret_pad, levels_o), F32),
            V((max(4 * ret_pad, 2 * fields + 16), max(row_count, columns)), BF),
            V((cells // base * ret_pad, base), BF),
            V((4 * field_pad, 128), F32),
            dma((4,)), dma((max(air_groups, sea_groups),)), dma((air_groups, pairs)),
        ]
        sends = ((9,), (4,), (max(air_groups, sea_groups),), (air_groups, pairs))
        vmem = pl.BlockSpec(memory_space=pltpu.VMEM)
        outs = (
            jax.ShapeDtypeStruct(air.shape, F32),
            jax.ShapeDtypeStruct(sea.shape, F32),
            jax.ShapeDtypeStruct((1, ret_fields, 1, columns), F32),
        )
        kept_outs = outs + (
            jax.ShapeDtypeStruct((cells // base * field_pad, base), F32),
            jax.ShapeDtypeStruct((128, 4 * field_pad), BF),
        )
        parts = pl.pallas_call(
            functools.partial(kernel, (groups, devs, air_groups, sends)),
            out_shape=kept_outs,
            in_specs=[pl.BlockSpec(memory_space=pltpu.HBM)] * 15,
            out_specs=(vmem,) * 5,
            scratch_shapes=scratch,
            compiler_params=pltpu.CompilerParams(
                collective_id=0, has_side_effects=True, vmem_limit_bytes=48 * 1024 * 1024),
            name="couple",
        )(*[pltpu.with_memory_space_constraint(x, pltpu.HBM) for x in args])
        air_next, sea_next, back = pl.pallas_call(
            functools.partial(finish, air_groups),
            out_shape=outs,
            in_specs=[vmem] * 5,
            out_specs=(pl.BlockSpec(memory_space=pl.ANY),) * 3,
            scratch_shapes=[V(sea.shape, F32), dma((6,))],
            compiler_params=pltpu.CompilerParams(vmem_limit_bytes=4 * 1024 * 1024),
            name="finish",
        )(*parts)
        return air_next, sea_next, back.transpose(0, 2, 1, 3)

    return jax.shard_map(
        on_device, mesh=mesh, in_specs=in_specs, out_specs=out_specs, check_vma=False)
```

time: 17.9 us -> 15.5 us (0.87)
  Pallas kernels: 17 us -> 14.7 us
    pallas_call x2, Pallas kernels: 17 us -> 14.7 us  [the longest x1 13.6 us: on_device(): pl.pallas_call(functools.partial(kernel, (groups, devs, air_groups, sends...]
where the time goes in v1:
time: 15.5 us; the launch traced here: 15.3 us
  Pallas kernels  14.7 us (95%)
  between operations  0.64 us (4%)
    pallas_call x1, Pallas kernels, on_device(): pl.pallas_call(functools.partial(kernel, (groups, devs, air_groups, sends...  13.6 us
    pallas_call x1, Pallas kernels, on_device(): pl.pallas_call(functools.partial(finish, air_groups), out_shape=outs, in_...  1.08 us

profile of v1, /device:TPU:24, one launch (start us, length us, event | category | flops | bytes accessed | tf_op | source)
XLA Modules:
  0.0 15.3 jit_solution(7482572793833631276)
XLA Ops:
  0.6 13.6 %couple.1 = (f32[1,1,128,1024]{3,2,1,0:T(8,128)S(1)}, f32[1,1,80,2048]{3,2,1,0:T(8,128)S(1)}, f32[1,12,1,1024]{3,2,1,0:T(1,128)S(1)}, f32[256,256]{1,0:T(8,128)S(1)}, bf16[128,128]{1,0:T(8,128)(2,1)S(1)}) custom-call(f32[1,1,128,1024]{3,2,1,0:T(8,128)} %refs_0_.1, s32[1,1,4,1024]{3,2,1,0:T(4,128)} %refs_1_.1, s32[1,1,256]{2,1,0:T(1,128)} %refs_2_.1, ...), custom_call_target="tpu_custom_call" | custom-call | tf_op jit(solution)/shard_map/couple/pallas_call | solution.py:635
  14.3 1.1 %finish.1 = (f32[1,1,128,1024]{3,2,1,0:T(8,128)}, f32[1,1,80,2048]{3,2,1,0:T(8,128)}, f32[1,12,1,1024]{3,2,1,0:T(1,128)}) custom-call(f32[1,1,128,1024]{3,2,1,0:T(8,128)S(1)} %get-tuple-element.11.a, f32[1,1,80,2048]{3,2,1,0:T(8,128)S(1)} %get-tuple-element.12.b, f32[1,12,1,1024]{3,2,1,0:T(1,128)S(1)} %get-tuple-element.13.c, ...), custom_call_target="tpu_custom_call" | custom-call | tf_op jit(solution)/shard_map/finish/pallas_call | solution.py:645

commit v2 on v1

--- a/solution.py
+++ b/solution.py
@@ -140,7 +140,7 @@
         anbr, asend, amix, fw, counts, mw, owner, recv, onbr, osend, omix, force, retw_in,
         pack, halo, gpack, ghalo, apool, gpool, opool, picker, amat, omat, member, ahead, early, lowmat, lowrow, spread, high,
         codes_out, codes_in, up_out, up_in, down_out, down_in, retw, slab, ret_bf, wide_force,
-        halo_recv, x_recv, up_recv,
+        halo_recv, x_recv, up_recv, told,
     ) = refs
     groups, devs, air_groups = sizes
     sea_groups = groups - air_groups
@@ -182,10 +182,15 @@
             for side in range(2)
         ]
 
-    def code_copy(s, o):
+    def code_copy(s):
         return pltpu.make_async_remote_copy(
-            src_ref=codes_out, dst_ref=codes_in.at[s], send_sem=x_send.at[o],
-            recv_sem=x_recv.at[s], device_id={"grp": air_groups + o})
+            src_ref=codes_out, dst_ref=codes_in.at[s], send_sem=x_send.at[0],
+            recv_sem=x_recv.at[s], device_id={"grp": air_groups})
+
+    def code_relay(s):
+        return pltpu.make_async_remote_copy(
+            src_ref=codes_in.at[s], dst_ref=codes_in.at[s], send_sem=x_send.at[air_groups + s],
+            recv_sem=x_recv.at[s], device_id={"grp": g + 1})
 
     def down_copy(s, o):
         return pltpu.make_async_remote_copy(
@@ -215,12 +220,11 @@
 
     @pl.when(is_air)
     def _():
-        for o in range(sea_groups):
-            pl.semaphore_signal(barrier, inc=1, device_id={"grp": air_groups + o})
+        pl.semaphore_signal(barrier, inc=1, device_id={"grp": air_groups})
         (l_asend, l_air, l_fw, l_owner, l_counts, l_anbr, l_amix, l_mw, l_sea) = loads(
             (asend_hbm, asend), (air_hbm, air_out), (fw_hbm, fw), (owner_hbm, owner), (counts_hbm, counts),
             (anbr_hbm, anbr), (amix_hbm, amix), (mw_hbm, mw), (sea_hbm, sea_out))
-        for c in (l_asend, l_fw, l_air, l_owner, l_counts, l_anbr, l_amix, l_mw):
+        for c in (l_asend, l_air, l_fw, l_anbr, l_counts, l_amix, l_mw, l_owner):
             c.start()
         neighbours = anbr.shape[2]
         excess = row_count - columns
@@ -237,17 +241,9 @@
         own = joined(mm(weight, top) + mm(weight, (state - top.astype(F32)).astype(BF)))
         own_parts = two_parts(own)
         packed(mm(own_parts, picker[:columns]).astype(BF), gpack, 2 * fields)
-        pl.semaphore_wait(barrier, 2 + sea_groups)
+        pl.semaphore_wait(barrier, 3)
         near_sides = halos(gpack, ghalo, 2 * fields, 2)
         for c in near_sides:
-            c.start()
-        packed(mm(top, picker[:columns]).astype(BF), pack, levels_a)
-        for h in range(columns // base_a):
-            at = slice(h * base_a, (h + 1) * base_a)
-            apool[:, at] = scaled(top[:, at], at.start, amat.shape[0], base_a, neighbours)
-            gpool[:, at] = scaled(own_parts[:, at], at.start, amat.shape[0], base_a, neighbours)
-        sides = halos(pack, halo, levels_a, 0)
-        for c in sides:
             c.start()
         l_owner.wait()
         owners = [owner[0, 0, 0, b] for b in range(blocks)]
@@ -262,14 +258,27 @@
             codes_out[b : b + 1, :] = jnp.full((1, 128), owners[b] * capacity + slots[b], I32)
         if codes_out.shape[0] > blocks:
             codes_out[blocks:, :] = jnp.full((codes_out.shape[0] - blocks, 128), -1, I32)
-        for o in range(sea_groups):
-            code_copy(mine, o).start()
+        code_copy(mine).start()
         l_sea.start()
 
-        l_counts.wait()
         l_anbr.wait()
         l_amix.wait()
         l_mw.wait()
+        for c in range(columns // width):
+            at = slice(c * width, (c + 1) * width)
+            counts_matrix(amat, high, [anbr[0, 0, k : k + 1, at] for k in range(neighbours)], base_a, at)
+        for h in range(columns // base_a):
+            at = slice(h * base_a, (h + 1) * base_a)
+            apool[:, at] = scaled(top[:, at], at.start, amat.shape[0], base_a, neighbours)
+            gpool[:, at] = scaled(own_parts[:, at], at.start, amat.shape[0], base_a, neighbours)
+        for c in range(columns // tile):
+            at = slice(c * tile, (c + 1) * tile)
+            mean = joined(mm(gpool[...], amat[:columns, at])) * (1.0 / neighbours)
+            here, mix = own[:, at], amix[0, :, at]
+            flux = here + mix * (mean - here)
+            slab[: 2 * fields, at] = two_parts(flux)
+            slab[2 * fields : 2 * fields + 16, at] = two_parts(jnp.broadcast_to(mix, (8, tile)))
+        l_counts.wait()
         column = row_columns(counts[...], row_count).astype(I32)
         low, high_of = column & (tile - 1), column >> (tile.bit_length() - 1)
         low_rows = as_rows(low, 16)
@@ -287,26 +296,16 @@
                 for i, h in enumerate(reach(p)):
                     member[h * tile + t * 16 : h * tile + (t + 1) * 16, at] = part * marks[i]
 
-        for c in range(columns // width):
-            at = slice(c * width, (c + 1) * width)
-            counts_matrix(amat, high, [anbr[0, 0, k : k + 1, at] for k in range(neighbours)], base_a, at)
-        for c in range(columns // tile):
-            at = slice(c * tile, (c + 1) * tile)
-            mean = joined(mm(gpool[...], amat[:columns, at])) * (1.0 / neighbours)
-            here, mix = own[:, at], amix[0, :, at]
-            flux = here + mix * (mean - here)
-            slab[: 2 * fields, at] = two_parts(flux)
-            slab[2 * fields : 2 * fields + 16, at] = two_parts(jnp.broadcast_to(mix, (8, tile)))
         for p in range(row_count // tile):
             at = slice(p * tile, (p + 1) * tile)
             ks = reach(p)
             ks = slice(ks[0] * tile, (ks[-1] + 1) * tile)
-            both = mm(slab[: 2 * fields + 16, ks], member[ks, at])
+            both = mm(jnp.concatenate([slab[: 2 * fields + 16, ks], amat[columns:, ks]], axis=0), member[ks, at])
             share = mw[0, :, at]
-            mix = joined(both[2 * fields :])[:1]
+            mix = joined(both[2 * fields : 2 * fields + 16])[:1]
             early[:fields, at] = joined(both[: 2 * fields]) * share
             early[fields : fields + 8, at] = jnp.broadcast_to(share * mix * (1.0 / neighbours), (8, tile))
-            ahead[:, at] = mm(amat[columns:, ks], member[ks, at]).astype(BF)
+            ahead[:, at] = both[2 * fields + 16 :].astype(BF)
         for c in near_sides:
             c.wait()
         far = jnp.concatenate([
@@ -317,8 +316,14 @@
             per = tile // block
             for q in range(per // 2):
                 b = slice(2 * q * block, (2 * q + 1) * block), slice((2 * q + 1) * block, (2 * q + 2) * block)
-                up_out[p * (per // 2) + q] = jnp.concatenate([values[:, b[0]], values[:, b[1]]], axis=0).astype(BF)
+                whole = fields - fields % 16
+                up_out[p * (per // 2) + q] = jnp.concatenate(
+                    [values[f, at] for f in (slice(whole), slice(whole, None)) for at in b], axis=0).astype(BF)
                 up_copy(mine, p * (per // 2) + q).start()
+        packed(mm(air_out[0, 0].astype(BF), picker[:columns]).astype(BF), pack, levels_a)
+        sides = halos(pack, halo, levels_a, 0)
+        for c in sides:
+            c.start()
         take_halo(sides, apool, levels_a, columns, neighbours)
         for c in range(columns // width):
             at = slice(c * width, (c + 1) * width)
@@ -340,21 +345,23 @@
             ratio = joined(sums[: 2 * ret_pad]) / joined(sums[2 * ret_pad :])
             for f in range(ret_fields):
                 back_out[0, f, :, at] = ratio[f : f + 1]
-        for o in range(sea_groups):
-            code_copy(mine, o).wait_send()
+        code_copy(mine).wait_send()
         for p in range(pairs):
             up_copy(mine, p).wait_send()
         l_sea.wait()
 
     @pl.when(jnp.logical_not(is_air))
     def _():
-        for s in range(air_groups):
-            pl.semaphore_signal(barrier, inc=1, device_id={"grp": s})
         not_first, not_last = mine > 0, mine < sea_groups - 1
 
         @pl.when(not_first)
         def _():
             pl.semaphore_signal(barrier, inc=1, device_id={"grp": g - 1})
+
+        @pl.when(jnp.logical_not(not_first))
+        def _():
+            for s in range(air_groups):
+                pl.semaphore_signal(barrier, inc=1, device_id={"grp": s})
 
         @pl.when(not_last)
         def _():
@@ -372,11 +379,20 @@
         l_sea.wait()
         top = sea_out[0, 0].astype(BF)
         packed(mm(top, picker[:cells]).astype(BF), pack, levels_o)
-        links = jnp.where(not_first, 1, 0) + jnp.where(not_last, 1, 0)
-        pl.semaphore_wait(barrier, 2 + air_groups + links)
+        links = jnp.where(not_first, 1, air_groups) + jnp.where(not_last, 1, 0)
+        pl.semaphore_wait(barrier, 2 + links)
         sides = halos(pack, halo, levels_o, 0)
         for c in sides:
             c.start()
+
+        @pl.when(not_first)
+        def _():
+            pl.semaphore_wait(told, 1)
+
+        @pl.when(not_last)
+        def _():
+            pl.semaphore_signal(told, inc=1, device_id={"grp": g + 1})
+
         l_air.start()
         l_retw.wait()
         l_recv.wait()
@@ -415,9 +431,9 @@
             down_copy(s, mine).start()
         wide_force[...] = jnp.zeros(wide_force.shape, F32)
         strong = force[...]
-        wide_force[:fields, :levels_o] = strong
-        wide_force[field_pad : field_pad + fields, :levels_o] = strong
-        wide_force[2 * field_pad : 2 * field_pad + fields, :levels_o] = strong - strong.astype(BF).astype(F32)
+        for i, part in enumerate((strong, strong, strong - strong.astype(BF).astype(F32))):
+            wide_force[i * field_pad : i * field_pad + fields, :levels_o] = part
+            wide_force[i * field_pad + fields : (i + 1) * field_pad, :levels_o] = part[fields - fields % 16 :]
         force_out[...] = wide_force[...].T.astype(BF)
         flux_out[...] = jnp.zeros(flux_out.shape, F32)
         back_out[...] = jnp.zeros(back_out.shape, F32)
@@ -440,19 +456,19 @@
             mean = mm(opool[:, cells:], omat[cells:, at]) * (1.0 / neighbours)
             sea_out[0, 0, :, at] += omix[0, :, at] * mean
 
-        def relay(p):
+        rows_high = []
+        whole = fields - fields % 16
+        zero = jnp.asarray(0, BF)
+        lines = lax.broadcasted_iota(I32, (16, block), 0)
+        side = [jnp.where((lines >= 8 * j) & (lines < 8 * j + 8), 1.0, 0.0).astype(BF) for j in range(2)]
+
+        def code():
+            @pl.when(jnp.logical_not(not_last))
+            def _():
+                for s in range(air_groups):
+                    code_relay(s).wait_recv()
+
             for s in range(air_groups):
-                relay_copy(s, p).wait_recv()
-
-                @pl.when(not_last)
-                def _():
-                    relay_copy(s, p).start()
-
-        rows_high = []
-
-        def code():
-            for s in range(air_groups):
-                code_copy(s, 0).wait_recv()
                 place = codes_in[s] - mine * capacity
                 ids = []
                 for b in range(blocks):
@@ -465,24 +481,25 @@
                         for k in range(capacity):
                             cell = jnp.where(here == k, recv[0, 0, k, s : s + 1, :], cell)
                     ids.append(jnp.where(held, cell, -1))
-                rows_high.append([i >> bits for i in ids])
+                rows_high.append([as_rows(i >> bits, 16) for i in ids])
                 if not same:
                     low = as_rows(jnp.concatenate(ids, axis=1) & (base - 1), 16)
                     for t in range(base // 16):
                         lowrow[t * 16 : (t + 1) * 16, s * row_span : (s + 1) * row_span] = low_hot(low, t)
 
-        def collect(p):
+        def collect(some):
             total = flux_out[...]
-            for s in range(air_groups):
-                arrived = up_in[s, p].astype(F32)
+            for s, p in some:
                 for j in range(2):
                     at = slice(s * row_span + (2 * p + j) * block, s * row_span + (2 * p + j + 1) * block)
-                    part = jnp.concatenate(
-                        [arrived[j * fields : (j + 1) * fields], jnp.zeros((field_pad - fields, block), F32)], axis=0)
-                    high_of = jnp.broadcast_to(rows_high[s][2 * p + j], (field_pad, block))
+                    high_of = rows_high[s][2 * p + j]
                     for h in range(highs):
-                        spread[h * field_pad : (h + 1) * field_pad, at] = (
-                            jnp.where(high_of == h, part, 0.0).astype(BF))
+                        held = high_of == jnp.asarray(h, BF)
+                        for f in range(whole // 16):
+                            spread[h * field_pad + f * 16 : h * field_pad + (f + 1) * 16, at] = jnp.where(
+                                held, up_in[s, p, j * whole + f * 16 : j * whole + (f + 1) * 16], zero)
+                        spread[h * field_pad + whole : (h + 1) * field_pad, at] = jnp.where(
+                            held, up_in[s, p, 2 * whole :] * side[j], zero)
                 at = slice(s * row_span + 2 * p * block, s * row_span + (2 * p + 2) * block)
                 total = total + lax.dot_general(spread[:, at], near[:, at], NT, preferred_element_type=F32)
             flux_out[...] = total
@@ -494,25 +511,46 @@
             if c + 1 < tiles:
                 build(c + 1)
         take_halo(sides, opool, levels_o, cells, neighbours)
+
+        @pl.when(not_last)
+        def _():
+            for s in range(air_groups):
+                code_relay(s).wait_recv()
+                code_relay(s).start()
+
         for c in range(late):
             rim(c)
+        order = [(s, p) for p in range(pairs) for s in reversed(range(air_groups))]
+
+        def relays(some):
+            @pl.when(not_last)
+            def _():
+                for s, p in some:
+                    relay_copy(s, p).wait_recv()
+                    relay_copy(s, p).start()
+
         for c in range(late, tiles):
             product(c, omat.shape[0])
             if c + 1 < tiles:
                 build(c + 1)
+        relays(order)
         code()
-        relay(0)
-        for p in range(pairs):
-            if p:
-                relay(p)
-            collect(p)
+        for n in range(0, len(order), 2):
+
+            @pl.when(jnp.logical_not(not_last))
+            def _():
+                for s, p in order[n : n + 2]:
+                    relay_copy(s, p).wait_recv()
+
+            collect(order[n : n + 2])
         for s in range(air_groups):
             down_copy(s, mine).wait_send()
 
         @pl.when(not_last)
         def _():
-            for p in range(pairs):
-                for s in range(air_groups):
+            for s in range(air_groups):
+                code_relay(s).wait_send()
+                for p in range(pairs):
                     relay_copy(s, p).wait_send()
 
         l_air.wait()
@@ -523,21 +561,29 @@
     base, field_pad = flux.shape[1], force.shape[1] // 4
     highs = flux.shape[0] // field_pad
     levels = b.shape[2]
-    first = pltpu.make_async_copy(a, a_out, sem.at[0])
-    last = pltpu.make_async_copy(c, c_out, sem.at[1])
-    first.start()
-    last.start()
+    lines = a.shape[2] // 4
+    early = [
+        pltpu.make_async_copy(a.at[0, 0, pl.ds(i * lines, lines)], a_out.at[0, 0, pl.ds(i * lines, lines)], sem.at[i])
+        for i in range(4)
+    ]
+    early.append(pltpu.make_async_copy(c, c_out, sem.at[4]))
+    for x in early:
+        x.start()
+    steps = 4 if highs % 4 == 0 else 1
 
     @pl.when(is_air)
     def _():
-        whole = pltpu.make_async_copy(b, b_out, sem.at[2])
-        whole.start()
-        whole.wait()
+        whole = []
+        for i in range(steps):
+            at = slice(i * highs // steps * base, (i + 1) * highs // steps * base)
+            whole.append(pltpu.make_async_copy(b.at[0, 0, :, at], b_out.at[0, 0, :, at], sem.at[5 + i]))
+            whole[-1].start()
+        for x in whole:
+            x.wait()
 
     @pl.when(jnp.logical_not(is_air))
     def _():
         copies = []
-        steps = 4 if highs % 4 == 0 else 1
         for i in range(steps):
             for h in range(i * highs // steps, (i + 1) * highs // steps):
                 at = slice(h * base, (h + 1) * base)
@@ -547,13 +593,13 @@
                 three = jnp.concatenate([top, rest, top], axis=0)
                 held[0, 0, :, at] = b[0, 0, :, at] + mm(force[:levels, : 3 * field_pad], three)
             at = slice(i * highs // steps * base, (i + 1) * highs // steps * base)
-            copies.append(pltpu.make_async_copy(held.at[0, 0, :, at], b_out.at[0, 0, :, at], sem.at[2 + i]))
+            copies.append(pltpu.make_async_copy(held.at[0, 0, :, at], b_out.at[0, 0, :, at], sem.at[5 + i]))
             copies[-1].start()
         for x in copies:
             x.wait()
 
-    first.wait()
-    last.wait()
+    for x in early:
+        x.wait()
 
 
 def solution(mesh):
@@ -619,9 +665,9 @@
             V((max(4 * ret_pad, 2 * fields + 16), max(row_count, columns)), BF),
             V((cells // base * ret_pad, base), BF),
             V((4 * field_pad, 128), F32),
-            dma((4,)), dma((max(air_groups, sea_groups),)), dma((air_groups, pairs)),
+            dma((4,)), dma((max(air_groups, sea_groups),)), dma((air_groups, pairs)), pltpu.SemaphoreType.REGULAR,
         ]
-        sends = ((9,), (4,), (max(air_groups, sea_groups),), (air_groups, pairs))
+        sends = ((9,), (4,), (2 * air_groups,), (air_groups, pairs))
         vmem = pl.BlockSpec(memory_space=pltpu.VMEM)
         outs = (
             jax.ShapeDtypeStruct(air.shape, F32),
@@ -647,7 +693,7 @@
             out_shape=outs,
             in_specs=[vmem] * 5,
             out_specs=(pl.BlockSpec(memory_space=pl.ANY),) * 3,
-            scratch_shapes=[V(sea.shape, F32), dma((6,))],
+            scratch_shapes=[V(sea.shape, F32), dma((9,))],
             compiler_params=pltpu.CompilerParams(vmem_limit_bytes=4 * 1024 * 1024),
             name="finish",
         )(*parts)

time: 15.5 us -> 14.8 us (0.955)
  Pallas kernels: 14.7 us -> 14 us
    pallas_call x1, Pallas kernels: 13.6 us -> 12.9 us  [on_device(): pl.pallas_call(functools.partial(kernel, (groups, devs, air_groups, sends...]
where the time goes in v2:
time: 14.8 us; the launch traced here: 14.6 us
  Pallas kernels  14 us (95%)
  between operations  0.64 us (4%)
    pallas_call x1, Pallas kernels, on_device(): pl.pallas_call(functools.partial(kernel, (groups, devs, air_groups, sends...  12.9 us
    pallas_call x1, Pallas kernels, on_device(): pl.pallas_call(functools.partial(finish, air_groups), out_shape=outs, in_...  1.11 us

profile of v2, /device:TPU:24, one launch (start us, length us, event | category | flops | bytes accessed | tf_op | source)
XLA Modules:
  0.0 14.6 jit_solution(9803241407980766409)
XLA Ops:
  0.6 12.9 %couple.1 = (f32[1,1,128,1024]{3,2,1,0:T(8,128)S(1)}, f32[1,1,80,2048]{3,2,1,0:T(8,128)S(1)}, f32[1,12,1,1024]{3,2,1,0:T(1,128)S(1)}, f32[256,256]{1,0:T(8,128)S(1)}, bf16[128,128]{1,0:T(8,128)(2,1)S(1)}) custom-call(f32[1,1,128,1024]{3,2,1,0:T(8,128)} %refs_0_.1, s32[1,1,4,1024]{3,2,1,0:T(4,128)} %refs_1_.1, s32[1,1,256]{2,1,0:T(1,128)} %refs_2_.1, ...), custom_call_target="tpu_custom_call" | custom-call | tf_op jit(solution)/shard_map/couple/pallas_call | solution.py:681
  13.5 1.1 %finish.1 = (f32[1,1,128,1024]{3,2,1,0:T(8,128)}, f32[1,1,80,2048]{3,2,1,0:T(8,128)}, f32[1,12,1,1024]{3,2,1,0:T(1,128)}) custom-call(f32[1,1,128,1024]{3,2,1,0:T(8,128)S(1)} %get-tuple-element.11.a, f32[1,1,80,2048]{3,2,1,0:T(8,128)S(1)} %get-tuple-element.12.b, f32[1,12,1,1024]{3,2,1,0:T(1,128)S(1)} %get-tuple-element.13.c, ...), custom_call_target="tpu_custom_call" | custom-call | tf_op jit(solution)/shard_map/finish/pallas_call | solution.py:691

commit v3 on v2

--- a/solution.py
+++ b/solution.py
@@ -535,14 +535,15 @@
                 build(c + 1)
         relays(order)
         code()
-        for n in range(0, len(order), 2):
+        groups_of = [order[n : n + 2] for n in range(0, len(order) - 2, 2)] + [[x] for x in order[-2:]]
+        for some in groups_of:
 
             @pl.when(jnp.logical_not(not_last))
             def _():
-                for s, p in order[n : n + 2]:
+                for s, p in some:
                     relay_copy(s, p).wait_recv()
 
-            collect(order[n : n + 2])
+            collect(some)
         for s in range(air_groups):
             down_copy(s, mine).wait_send()
 

time: 14.8 us -> 14.9 us (level)
  no operation moved by 1% of the time
where the time goes in v3:
time: 14.9 us; the launch traced here: 14.7 us
  Pallas kernels  14.1 us (95%)
  between operations  0.64 us (4%)
    pallas_call x1, Pallas kernels, on_device(): pl.pallas_call(functools.partial(kernel, (groups, devs, air_groups, sends...  13 us
    pallas_call x1, Pallas kernels, on_device(): pl.pallas_call(functools.partial(finish, air_groups), out_shape=outs, in_...  1.11 us

profile of v3, /device:TPU:24, one launch (start us, length us, event | category | flops | bytes accessed | tf_op | source)
XLA Modules:
  0.0 14.7 jit_solution(2876970803941427319)
XLA Ops:
  0.6 13.0 %couple.1 = (f32[1,1,128,1024]{3,2,1,0:T(8,128)S(1)}, f32[1,1,80,2048]{3,2,1,0:T(8,128)S(1)}, f32[1,12,1,1024]{3,2,1,0:T(1,128)S(1)}, f32[256,256]{1,0:T(8,128)S(1)}, bf16[128,128]{1,0:T(8,128)(2,1)S(1)}) custom-call(f32[1,1,128,1024]{3,2,1,0:T(8,128)} %refs_0_.1, s32[1,1,4,1024]{3,2,1,0:T(4,128)} %refs_1_.1, s32[1,1,256]{2,1,0:T(1,128)} %refs_2_.1, ...), custom_call_target="tpu_custom_call" | custom-call | tf_op jit(solution)/shard_map/couple/pallas_call | solution.py:682
  13.6 1.1 %finish.1 = (f32[1,1,128,1024]{3,2,1,0:T(8,128)}, f32[1,1,80,2048]{3,2,1,0:T(8,128)}, f32[1,12,1,1024]{3,2,1,0:T(1,128)}) custom-call(f32[1,1,128,1024]{3,2,1,0:T(8,128)S(1)} %get-tuple-element.11.a, f32[1,1,80,2048]{3,2,1,0:T(8,128)S(1)} %get-tuple-element.12.b, f32[1,12,1,1024]{3,2,1,0:T(1,128)S(1)} %get-tuple-element.13.c, ...), custom_call_target="tpu_custom_call" | custom-call | tf_op jit(solution)/shard_map/finish/pallas_call | solution.py:692
